TPU v7x, 32 devices: a whole 2x2x4 slice. The times are simulated.
32 devices in a mesh: grp: 2 (over y), lat: 4 (over z), lay: 4 (over x, core).
Axes of the slice: x: 2, y: 2, z: 4, core: 2. Of those that a mesh axis runs over, the one named last changes fastest.
Arguments:
- acts: bfloat16 [128, 4, 1280], P(('grp', 'lat'), 'lay'), parts along dimension 0, may hold values from -6 to 6
- w_enc: bfloat16 [4, 1280, 1536], P('lay', None, 'lat'), may hold values from -0.078125 to 0.078125
- w_dec: bfloat16 [1536, 4, 1280], P('lat', 'lay'), may hold values from -0.15625 to 0.15625
- b_enc: float32 [1536], P('lat'), may hold values from -3 to 3
- b_dec: float32 [4, 1280], P('lay'), may hold values from -3 to 3
Outputs:
- lat_grad: bfloat16 [128, 1536], P('grp', 'lat'), parts along dimension 0
- enc_grad: bfloat16 [8, 1280, 1536], P(('grp', 'lay'), None, 'lat'), parts along dimension 0
- dec_grad: bfloat16 [1536, 8, 1280], P('lat', ('grp', 'lay')), parts along dimension 1
There are 2 independent parts, one for each index of `grp`. A program takes and returns all parts, laid end to end along the dimension named above; an argument that names none is the same for every part. Nothing has to cross between parts.
All inputs are finite; a program needn't handle non-finite values.
Results may differ from a plain program's by a relative error of at most 0.023.
Values may be sent and summed in bfloat16 or wider, within the bound.
A program may use at most 64 MiB of HBM per device.

v0:
```python
import jax
import jax.numpy as jnp
from jax import lax
from jax.sharding import PartitionSpec as P


def on_device(acts, w_enc, w_dec, b_enc, b_dec):
    row_dev, lay_dev, width = acts.shape
    lat_dev = w_enc.shape[2]
    gathered = lax.all_gather(acts, "lat", axis=0, tiled=True)
    term = jnp.einsum("bld,ldm->bm", gathered, w_enc, preferred_element_type=jnp.float32)
    pre = lax.psum(term.astype(jnp.bfloat16), "lay").astype(jnp.float32) + b_enc[None, :]
    code = (jax.nn.softplus(4.0 * pre) / 4.0).astype(jnp.bfloat16)
    slope = jax.nn.sigmoid(4.0 * pre)
    w_flat = w_dec.reshape(lat_dev, lay_dev * width)
    mine = lax.psum_scatter(
        jnp.dot(code, w_flat, preferred_element_type=jnp.float32).astype(jnp.bfloat16),
        "lat",
        scatter_dimension=0,
        tiled=True,
    ).astype(jnp.float32)
    recon = mine.reshape(row_dev, lay_dev, width)
    err_own = (recon + b_dec[None, :, :] - acts.astype(jnp.float32)).astype(jnp.bfloat16)
    err_all = lax.all_gather(err_own, "lat", axis=0, tiled=True)
    back = jnp.einsum("bld,mld->bm", err_all, w_dec, preferred_element_type=jnp.float32)
    back_total = lax.psum(back.astype(jnp.bfloat16), "lay").astype(jnp.float32)
    lat_grad = (back_total * slope).astype(jnp.bfloat16)
    enc_grad = jnp.einsum(
        "bld,bm->ldm", gathered, lat_grad, preferred_element_type=jnp.float32
    ).astype(jnp.bfloat16)
    dec_grad = jnp.einsum("bm,bld->mld", code, err_all, preferred_element_type=jnp.float32).astype(
        jnp.bfloat16
    )
    return (lat_grad, enc_grad, dec_grad)


def solution(mesh):
    in_specs = (
        P(("grp", "lat"), "lay", None),
        P("lay", None, "lat"),
        P("lat", "lay", None),
        P("lat"),
        P("lay", None),
    )
    out_specs = (P("grp", "lat"), P(("grp", "lay"), None, "lat"), P("lat", ("grp", "lay"), None))
    return jax.shard_map(
        on_device, mesh=mesh, in_specs=in_specs, out_specs=out_specs, check_vma=False
    )
```

profile of v0, /device:TPU:0, one launch (start us, length us, event | category | flops | bytes accessed | tf_op | source)
XLA Modules:
  0.0 92.7 jit_solution(12890388767885433730)
XLA Ops:
  7.2 0.0 copy-start
  7.2 0.0 copy-start.3
  7.2 0.0 reduce-scatter.2.cloned.1.call-start
  7.2 15.5 %all_gather.6 = bf16[64,1,1280]{2,0,1:T(8,128)(2,1)S(1)} all-gather(bf16[16,1,1280]{2,0,1:T(8,128)(2,1)} %param.5), channel_id=1, replica_groups=mesh['grp'=2,'lat'=4,'lay'=4] {'lat'}, dimensions={0}, use_global_device_ids=true | all-gather | bytes 204800 | tf_op jit(solution)/shard_map/all_gather | solution.py:10
  22.8 1.5 %convolution_convert_fusion.4 = bf16[64,384]{1,0:T(8,128)(2,1)S(1)} fusion(bf16[1,1280,384]{2,1,0:T(8,128)(2,1)} %param.6, bf16[64,1,1280]{2,0,1:T(8,128)(2,1)S(1)} %all_gather.6), kind=kOutput, calls=%fused_computation.6 | convolution fusion | flops 62939136 | bytes 1196032 | tf_op jit(solution)/shard_map/bld,ldm->bm/dot_general | solution.py:11
  24.2 0.0 copy-start.4
  24.3 0.0 copy-start.2
  24.3 10.7 %psum.14 = bf16[64,384]{1,0:T(8,128)(2,1)S(1)} all-reduce(bf16[64,384]{1,0:T(8,128)(2,1)S(1)} %convolution_convert_fusion.4), channel_id=1, replica_groups=mesh['grp'=2,'lat'=4,'lay'=4] {'lay'}, use_global_device_ids=true, to_apply=%region_0.0 | all-reduce | flops 24576 | bytes 98304 | tf_op jit(solution)/shard_map/psum | solution.py:12
  34.9 0.0 copy-done
  34.9 0.0 copy-done.3
  34.9 1.0 %convolution_convert_fusion.2 = bf16[64,1280]{1,0:T(8,128)(2,1)} fusion(bf16[384,1,1280]{2,0,1:T(8,128)(2,1)S(1)} %copy-done, bf16[64,384]{1,0:T(8,128)(2,1)S(1)} %psum.14, f32[384]{0:T(512)S(1)} %copy-done.3), kind=kOutput, calls=%fused_computation.4 | convolution fusion | flops 63266816 | bytes 1197568 | tf_op jit(solution)/shard_map/dot_general | solution.py:17
  35.9 0.0 reduce-scatter.2.cloned.1.call-update
  35.9 0.0 copy-done.4
  36.0 21.4 %reduce-scatter.2.cloned.1.call-done = bf16[16,1280]{1,0:T(8,128)(2,1)} async-done(((bf16[64,1280]{1,0:T(8,128)(2,1)}), bf16[16,1280]{1,0:T(8,128)(2,1)}) %reduce-scatter.2.cloned.1.call-update) | async-done | bytes 40976 | tf_op jit(solution)/shard_map/reduce_scatter | solution.py:16
  57.3 0.0 copy-done.2
  57.3 0.8 fusion.11
  58.1 13.5 %all_gather.7 = bf16[64,1,1280]{2,0,1:T(8,128)(2,1)S(1)} all-gather(bf16[16,1,1280]{2,0,1:T(8,128)(2,1)S(1)} %fusion.11), channel_id=1, replica_groups=mesh['grp'=2,'lat'=4,'lay'=4] {'lat'}, dimensions={0}, use_global_device_ids=true | all-gather | bytes 204800 | tf_op jit(solution)/shard_map/all_gather | solution.py:24
  71.6 0.4 convolution_convert_fusion.3
  72.0 1.4 %fusion.1 = bf16[384,1,1280]{2,0,1:T(8,128)(2,1)} fusion(bf16[64,1,1280]{2,0,1:T(8,128)(2,1)S(1)} %all_gather.7, bf16[64,384]{1,0:T(8,128)(2,1)S(1)} %psum.14, f32[384]{0:T(512)S(1)} %copy-done.3), kind=kOutput, calls=%fused_computation.3 | convolution fusion | flops 63676416 | bytes 1197568 | tf_op jit(solution)/shard_map/bm,bld->mld/dot_general | solution.py:31
  73.5 10.5 %psum.15 = bf16[64,384]{1,0:T(8,128)(2,1)S(1)} all-reduce(bf16[64,384]{1,0:T(8,128)(2,1)S(1)} %convolution_convert_fusion.3), channel_id=1, replica_groups=mesh['grp'=2,'lat'=4,'lay'=4] {'lay'}, use_global_device_ids=true, to_apply=%region_2.3 | all-reduce | flops 24576 | bytes 98304 | tf_op jit(solution)/shard_map/psum | solution.py:26
  84.0 0.0 copy-start.1
  84.1 0.4 fusion
  84.5 1.3 %copy.8 = bf16[1,1280,384]{2,1,0:T(8,128)(2,1)} copy(bf16[1,1280,384]{1,2,0:T(8,128)(2,1)S(1)} %fusion) | data formatting | bytes 1966080
  85.8 0.0 copy-done.1
  (2 shorter events, 0.1 us)
Async XLA Ops:
  7.2 27.8 %copy-start = (bf16[384,1,1280]{2,0,1:T(8,128)(2,1)S(1)}, bf16[384,1,1280]{2,0,1:T(8,128)(2,1)}, u32[]{:S(2)}) copy-start(bf16[384,1,1280]{2,0,1:T(8,128)(2,1)} %param.7) | copy-start | bytes 2949124
  7.2 27.8 %copy-start.3 = (f32[384]{0:T(512)S(1)}, f32[384]{0:T(512)}, u32[]{:S(2)}) copy-start(f32[384]{0:T(512)} %param.8) | copy-start | bytes 4612
  7.2 50.2 %reduce-scatter.2.cloned.1.call-start = ((), (), s32[]{:S(2)}) async-start(), calls=%async_computation.1 | async-start | bytes 204800 | tf_op jit(solution)/shard_map/reduce_scatter | solution.py:16
  24.2 11.7 %copy-start.4 = (f32[1,1280]{1,0:T(1,128)S(1)}, f32[1,1280]{1,0:T(1,128)}, u32[]{:S(2)}) copy-start(f32[1,1280]{1,0:T(1,128)} %param.9) | copy-start | bytes 15364
  24.3 33.1 %copy-start.2 = (bf16[16,1,1280]{2,0,1:T(8,128)(2,1)S(1)}, bf16[16,1,1280]{2,0,1:T(8,128)(2,1)}, u32[]{:S(2)}) copy-start(bf16[16,1,1280]{2,0,1:T(8,128)(2,1)} %param.5) | copy-start | bytes 122884
  84.0 1.8 %copy-start.1 = (bf16[64,384]{1,0:T(8,128)(2,1)}, bf16[64,384]{1,0:T(8,128)(2,1)S(1)}, u32[]{:S(2)}) copy-start(bf16[64,384]{1,0:T(8,128)(2,1)S(1)} %multiply_convert_fusion) | copy-start | bytes 147460
Sparse Core Ops, SparseCore 0:
  36.1 21.2 reduce-scatter.1
where the time goes:
time: 93 us; the launch traced here: 92.7 us
  blocking collectives  50.1 us (54%)
  waiting for transfers between devices  21.4 us (23%)
  between operations  14.1 us (15%)
  matrix products  4.76 us (5%)
  local copies, waits for them, and re-layouts  1.35 us (1%)
    reduce_scatter x1, waiting for transfers between devices, on_device(): lax.psum_scatter(jnp.dot(code, w_flat, preferred_element_type=jnp.float32...  21.4 us
    all_gather x1, blocking collectives, on_device(): gathered = lax.all_gather(acts, 'lat', axis=0, tiled=True)  15.5 us
    all_gather x1, blocking collectives, on_device(): err_all = lax.all_gather(err_own, 'lat', axis=0, tiled=True)  13.5 us
    psum x1, blocking collectives, on_device(): lax.psum(term.astype(jnp.bfloat16), 'lay').astype(jnp.float32)  10.7 us
    psum x1, blocking collectives, on_device(): back_total = lax.psum(back.astype(jnp.bfloat16), 'lay').astype(jnp.float32)  10.5 us
  transfers between devices with their start and end apart: 1, of which 1 were waited for; matrix products, arithmetic and copies ran while one was open for 0% of the time, Pallas kernels for 0%

commit v1 on v0

v1 whole, which is shorter than its diff:
```python
import functools

import jax
import jax.numpy as jnp
from jax import lax
from jax.experimental import pallas as pl
from jax.experimental.pallas import tpu as pltpu
from jax.sharding import PartitionSpec as P

MESH = pl.DeviceIdType.MESH
F32, BF16 = jnp.float32, jnp.bfloat16
NT = (((1,), (1,)), ((), ()))


def step(
    n_lat, n_lay, acts_hbm, wenc_hbm, wdec_hbm, benc_ref, bdec_ref, lat_out, enc_out, dec_out,
    acts_all, wenc, wdec, pre_buf, back_buf, rec_mine, rec_buf, err_all,
    load, acts_s, acts_r, pre_s, pre_r, rec_s, rec_r, err_s, err_r, back_s, back_r,
):
    z, l = lax.axis_index("lat"), lax.axis_index("lay")
    row_dev, wide = acts_all.shape[1:]
    rows, lat_dev = n_lat * row_dev, wenc.shape[1]

    load_acts = pltpu.make_async_copy(acts_hbm, acts_all.at[z], load.at[0])
    load_enc = pltpu.make_async_copy(wenc_hbm, wenc, load.at[1])
    load_dec = pltpu.make_async_copy(wdec_hbm, wdec, load.at[2])
    load_acts.start()
    load_enc.start()
    load_dec.start()

    def lat_peer(k):
        return {"lat": lax.rem(z + k, n_lat)}

    def lay_peer(k):
        return {"lay": lax.rem(l + k, n_lay)}

    barrier = pltpu.get_barrier_semaphore()
    for k in range(1, n_lat):
        pl.semaphore_signal(barrier, inc=1, device_id=lat_peer(k), device_id_type=MESH)
    for k in range(1, n_lay):
        pl.semaphore_signal(barrier, inc=1, device_id=lay_peer(k), device_id_type=MESH)
    pl.semaphore_wait(barrier, n_lat + n_lay - 2)

    def send(src, dst, send_sem, recv_sem, peer):
        copy = pltpu.make_async_remote_copy(
            src_ref=src, dst_ref=dst, send_sem=send_sem, recv_sem=recv_sem,
            device_id=peer, device_id_type=MESH,
        )
        copy.start()
        return copy

    started = []

    def to_lat(buf, sent, received, src=None):
        copies = []
        for k in range(1, n_lat):
            block = buf.at[z] if src is None else src.at[lax.rem(z + k, n_lat)]
            copies.append(send(block, buf.at[z], sent.at[k], received.at[k], lat_peer(k)))
        started.extend(copies)
        return copies

    def to_lay(buf, sent, received):
        copies = [
            send(buf.at[l], buf.at[l], sent.at[k], received.at[k], lay_peer(k))
            for k in range(1, n_lay)
        ]
        started.extend(copies)
        return copies

    def total(buf):
        whole = buf[0].astype(F32)
        for i in range(1, n_lay):
            whole += buf[i].astype(F32)
        return whole

    load_acts.wait()
    copies = to_lat(acts_all, acts_s, acts_r)
    load_enc.wait()
    for copy in copies:
        copy.wait_recv()
    acts = acts_all[...].reshape(rows, wide)
    pre_buf[l] = jnp.dot(acts, wenc[...], preferred_element_type=F32).astype(BF16)
    copies = to_lay(pre_buf, pre_s, pre_r)
    load_dec.wait()
    for copy in copies:
        copy.wait_recv()
    x = 4.0 * (total(pre_buf) + benc_ref[...].reshape(1, lat_dev))
    e = jnp.exp(-jnp.abs(x))
    code = (0.25 * (jnp.maximum(x, 0.0) + jnp.log1p(e))).astype(BF16)
    rec_mine[...] = (
        jnp.dot(code, wdec[...], preferred_element_type=F32).astype(BF16).reshape(rec_mine.shape)
    )
    copies = to_lat(rec_buf, rec_s, rec_r, rec_mine)
    slope = jnp.where(x >= 0.0, 1.0, e) / (1.0 + e)
    acts_t = acts.astype(F32).T.astype(BF16)
    code_t = code.astype(F32).T.astype(BF16)
    err = bdec_ref[...] - acts_all[z].astype(F32) + rec_mine[z].astype(F32)
    for k, copy in enumerate(copies, 1):
        copy.wait_recv()
        err += rec_buf[lax.rem(z + n_lat - k, n_lat)].astype(F32)
    err_all[z] = err.astype(BF16)
    copies = to_lat(err_all, err_s, err_r)
    for copy in copies:
        copy.wait_recv()
    errs = err_all[...].reshape(rows, wide)
    back_buf[l] = lax.dot_general(errs, wdec[...], NT, preferred_element_type=F32).astype(BF16)
    copies = to_lay(back_buf, back_s, back_r)
    dec_out[...] = jnp.dot(code_t, errs, preferred_element_type=F32).astype(BF16)
    for copy in copies:
        copy.wait_recv()
    lat_grad = (total(back_buf) * slope).astype(BF16)
    lat_out[...] = lat_grad
    enc_out[...] = jnp.dot(acts_t, lat_grad, preferred_element_type=F32).astype(BF16)
    for copy in started:
        copy.wait_send()


def solution(mesh):
    n_lat, n_lay = mesh.shape["lat"], mesh.shape["lay"]

    def on_device(acts, w_enc, w_dec, b_enc, b_dec):
        row_dev, lay_dev, width = acts.shape
        lat_dev = w_enc.shape[2]
        wide, rows = lay_dev * width, n_lat * row_dev
        hbm = pl.BlockSpec(memory_space=pltpu.HBM)
        vmem = pl.BlockSpec(memory_space=pltpu.VMEM)
        dma = pltpu.SemaphoreType.DMA
        lat_grad, enc_grad, dec_grad = pl.pallas_call(
            functools.partial(step, n_lat, n_lay),
            out_shape=[
                jax.ShapeDtypeStruct((rows, lat_dev), BF16),
                jax.ShapeDtypeStruct((wide, lat_dev), BF16),
                jax.ShapeDtypeStruct((lat_dev, wide), BF16),
            ],
            in_specs=[hbm, hbm, hbm, vmem, vmem],
            out_specs=[vmem, vmem, vmem],
            scratch_shapes=[
                pltpu.VMEM((n_lat, row_dev, wide), BF16),
                pltpu.VMEM((wide, lat_dev), BF16),
                pltpu.VMEM((lat_dev, wide), BF16),
                pltpu.VMEM((n_lay, rows, lat_dev), BF16),
                pltpu.VMEM((n_lay, rows, lat_dev), BF16),
                pltpu.VMEM((n_lat, row_dev, wide), BF16),
                pltpu.VMEM((n_lat, row_dev, wide), BF16),
                pltpu.VMEM((n_lat, row_dev, wide), BF16),
                dma((3,)),
                dma((n_lat,)), dma((n_lat,)),
                dma((n_lay,)), dma((n_lay,)),
                dma((n_lat,)), dma((n_lat,)),
                dma((n_lat,)), dma((n_lat,)),
                dma((n_lay,)), dma((n_lay,)),
            ],
            compiler_params=pltpu.CompilerParams(collective_id=0, has_side_effects=True),
            cost_estimate=pl.CostEstimate(
                flops=10 * rows * wide * lat_dev,
                bytes_accessed=8 * wide * lat_dev,
                transcendentals=0,
            ),
        )(
            acts.reshape(row_dev, wide),
            w_enc.reshape(wide, lat_dev),
            w_dec.reshape(lat_dev, wide),
            b_enc,
            b_dec.reshape(1, wide),
        )
        return (
            lat_grad,
            enc_grad.reshape(lay_dev, width, lat_dev),
            dec_grad.reshape(lat_dev, lay_dev, width),
        )

    in_specs = (
        P(("grp", "lat"), "lay", None),
        P("lay", None, "lat"),
        P("lat", "lay", None),
        P("lat"),
        P("lay", None),
    )
    out_specs = (P("grp", "lat"), P(("grp", "lay"), None, "lat"), P("lat", ("grp", "lay"), None))
    return jax.shard_map(
        on_device, mesh=mesh, in_specs=in_specs, out_specs=out_specs, check_vma=False
    )
```

time: 93 us -> 35.9 us (0.39)
  blocking collectives: 50.1 us -> 0 us
  Pallas kernels: 0 us -> 30.3 us
  waiting for transfers between devices: 21.4 us -> 0 us
  between operations: 14.1 us -> 0.64 us
  matrix products: 4.76 us -> 0 us
  local copies, waits for them, and re-layouts: 1.35 us -> 4.7 us
    pallas_call x0 -> x1, Pallas kernels: none -> 30.3 us  [on_device(): pl.pallas_call(functools.partial(step, n_lat, n_lay), out_shape=[jax.Shap...]
    all_gather x2 -> x0, blocking collectives: 29 us -> none  [the longest x1 15.5 us: on_device(): gathered = lax.all_gather(acts, 'lat', axis=0, tiled=True)]
    reduce_scatter x1 -> x0, waiting for transfers between devices: 21.4 us -> none  [on_device(): lax.psum_scatter(jnp.dot(code, w_flat, preferred_element_type=jnp.float32...]
    psum x2 -> x0, blocking collectives: 21.2 us -> none  [the longest x1 10.7 us: on_device(): lax.psum(term.astype(jnp.bfloat16), 'lay').astype(jnp.float32)]
    dot_general x5 -> x0, matrix products: 4.76 us -> none  [the longest x1 1.48 us: on_device(): jnp.einsum('bld,ldm->bm', gathered, w_enc, preferred_element_type=jnp.flo...]
    unnamed x11 -> x5, local copies, waits for them, and re-layouts: 1.35 us -> 4.7 us
  transfers between devices with their start and end apart: 1 -> 0, of which waited for: 1 -> 0; matrix products, arithmetic and copies ran while one was open for 0% -> 0% of each run, Pallas kernels for 0% -> 0%
where the time goes in v1:
time: 35.9 us; the launch traced here: 35.6 us
  Pallas kernels  30.3 us (84%)
  local copies, waits for them, and re-layouts  4.7 us (13%)
  between operations  0.64 us (2%)
    pallas_call x1, Pallas kernels, on_device(): pl.pallas_call(functools.partial(step, n_lat, n_lay), out_shape=[jax.Shap...  30.3 us
    unnamed x5, local copies, waits for them, and re-layouts  4.7 us

profile of v1, /device:TPU:0, one launch (start us, length us, event | category | flops | bytes accessed | tf_op | source)
XLA Modules:
  0.0 35.6 jit_solution(10600102391357578625)
XLA Ops:
  0.6 30.3 %shard_map.76 = (bf16[64,384]{1,0:T(8,128)(2,1)}, bf16[1280,384]{1,0:T(8,128)(2,1)}, bf16[384,1280]{1,0:T(8,128)(2,1)}) custom-call(bf16[16,1280]{1,0:T(8,128)(2,1)} %bitcast.9, bf16[1280,384]{1,0:T(8,128)(2,1)} %bitcast.5, bf16[384,1280]{1,0:T(8,128)(2,1)} %bitcast.6, f32[384]{0:T(512)} %benc_ref.1, f32[1,1280]{1,0:T(1,128)} %bdec_ref.1), custom_call_target="tpu_custom_call" | custom-call | flops 314572800 | bytes 3932160 | tf_op jit(solution)/shard_map/pallas_call | solution.py:128
  30.9 1.4 %copy.11 = bf16[64,384]{1,0:T(8,128)(2,1)} copy(bf16[64,384]{1,0:T(8,128)(2,1)} %get-tuple-element.12) | data formatting | bytes 98304
  32.4 0.0 copy-start
  32.4 2.3 %copy.12 = bf16[1,1280,384]{2,1,0:T(8,128)(2,1)} copy(bf16[1,1280,384]{2,1,0:T(8,128)(2,1)} %bitcast.8) | data formatting | bytes 1966080
  34.7 0.0 copy-done
  34.7 0.9 %copy.13 = bf16[384,1,1280]{2,0,1:T(8,128)(2,1)} copy(bf16[384,1,1280]{2,0,1:T(8,128)(2,1)S(1)} %bitcast.7) | data formatting | bytes 1966080
Async XLA Ops:
  32.4 2.3 %copy-start = (bf16[384,1280]{1,0:T(8,128)(2,1)S(1)}, bf16[384,1280]{1,0:T(8,128)(2,1)}, u32[]{:S(2)}) copy-start(bf16[384,1280]{1,0:T(8,128)(2,1)} %get-tuple-element.8) | copy-start | bytes 2949124

commit v2 on v1

v2 whole, which is shorter than its diff:
```python
import functools

import jax
import jax.numpy as jnp
from jax import lax
from jax.experimental import pallas as pl
from jax.experimental.pallas import tpu as pltpu
from jax.sharding import PartitionSpec as P

MESH = pl.DeviceIdType.MESH
F32, BF16 = jnp.float32, jnp.bfloat16


def flip(v, j):
    out, bit = v, 1
    while bit <= j:
        if j & bit:
            out = out + bit * (1 - 2 * lax.rem(lax.div(v, bit), 2))
        bit *= 2
    return out


def step(
    n_lat, n_lay, groups, acts_hbm, wenc_hbm, wdec_hbm, benc_ref, bdec_ref,
    lat_out, acts_t, dec_out,
    acts_all, wenc, wdec, wdec_t, pre_buf, back_buf, rec_mine, rec_buf, err_all, code_all, slope,
    load, acts_s, acts_r, pre_s, pre_r, rec_s, rec_r, err_s, err_r, back_s, back_r,
):
    z, l = lax.axis_index("lat"), lax.axis_index("lay")
    row_dev, wide = acts_all.shape[1:]
    rows, lat_dev = n_lat * row_dev, wenc.shape[1]
    size = n_lat // groups
    part = size * row_dev

    load_acts = pltpu.make_async_copy(acts_hbm, acts_all.at[z], load.at[0])
    load_enc = pltpu.make_async_copy(wenc_hbm, wenc, load.at[1])
    load_dec = pltpu.make_async_copy(wdec_hbm, wdec, load.at[2])
    load_acts.start()
    load_enc.start()
    load_dec.start()

    if groups > 1:
        dest = source = lambda j: flip(z, j)
    else:
        dest = lambda j: lax.rem(z + j, n_lat)
        source = lambda j: lax.rem(z + n_lat - j, n_lat)
    group = [flip(lax.div(z, size), g) if groups > 1 else 0 for g in range(groups)]

    def lay_peer(k):
        return {"lay": lax.rem(l + k, n_lay)}

    barrier = pltpu.get_barrier_semaphore()
    for j in reversed(range(1, n_lat)):
        pl.semaphore_signal(
            barrier, inc=1, device_id={"lat": dest(j)}, device_id_type=MESH
        )
    for k in range(1, n_lay):
        pl.semaphore_signal(barrier, inc=1, device_id=lay_peer(k), device_id_type=MESH)
    pl.semaphore_wait(barrier, n_lat + n_lay - 2)

    started = []

    def send(src, dst, send_sem, recv_sem, peer):
        copy = pltpu.make_async_remote_copy(
            src_ref=src, dst_ref=dst, send_sem=send_sem, recv_sem=recv_sem,
            device_id=peer, device_id_type=MESH,
        )
        copy.start()
        started.append(copy)
        return copy

    def to_lat(buf, sent, received):
        return {
            j: send(buf.at[z], buf.at[z], sent.at[j], received.at[j], {"lat": dest(j)})
            for j in reversed(range(1, n_lat))
        }

    def to_lay(buf, g, sent, received):
        block = buf.at[l, group[g]]
        return [
            send(block, block, sent.at[g, k], received.at[g, k], lay_peer(k))
            for k in range(1, n_lay)
        ]

    def arrive(copies, g):
        for j in range(g * size, (g + 1) * size):
            if j:
                copies[j].wait_recv()

    def rows_of(buf, g):
        return buf[pl.ds(group[g] * size, size)].reshape(part, wide)

    def total(buf, g):
        whole = buf[0, group[g]].astype(F32)
        for i in range(1, n_lay):
            whole += buf[i, group[g]].astype(F32)
        return whole

    load_acts.wait()
    acts_copies = to_lat(acts_all, acts_s, acts_r)
    load_enc.wait()
    pre_copies, rec_copies = {}, {}

    def encode(g):
        arrive(acts_copies, g)
        pre = jnp.dot(rows_of(acts_all, g), wenc[...], preferred_element_type=F32)
        pre_buf[l, group[g]] = pre.astype(BF16)
        pre_copies[g] = to_lay(pre_buf, g, pre_s, pre_r)

    def decode(g):
        for copy in pre_copies[g]:
            copy.wait_recv()
        x = 4.0 * (total(pre_buf, g) + benc_ref[...].reshape(1, lat_dev))
        e = jnp.exp(-jnp.abs(x))
        code = (0.25 * (jnp.maximum(x, 0.0) + jnp.log1p(e))).astype(BF16)
        rec = jnp.dot(code, wdec[...], preferred_element_type=F32).astype(BF16)
        rec_mine[pl.ds(group[g] * size, size)] = rec.reshape(size, row_dev, wide)
        for j in range(g * size, (g + 1) * size):
            if j:
                rec_copies[j] = send(
                    rec_mine.at[dest(j)], rec_buf.at[z], rec_s.at[j], rec_r.at[j],
                    {"lat": dest(j)},
                )
        code_all[group[g]] = code
        slope[group[g]] = jnp.where(x >= 0.0, 1.0, e) / (1.0 + e)

    for g in range(groups):
        if g == groups - 1 and g:
            decode(0)
        encode(g)
        if g == 0:
            load_dec.wait()
            wdec_t[...] = wdec[...].astype(F32).T.astype(BF16)
    for g in range(1 if groups > 1 else 0, groups):
        decode(g)
    acts_t[...] = acts_all[...].reshape(rows, wide).astype(F32).T.astype(BF16)
    code_t = code_all[...].reshape(rows, lat_dev).astype(F32).T.astype(BF16)
    err = bdec_ref[...] - acts_all[z].astype(F32) + rec_mine[z].astype(F32)
    for j in range(1, n_lat):
        rec_copies[j].wait_recv()
        err += rec_buf[source(j)].astype(F32)
    err_all[z] = err.astype(BF16)
    err_copies = to_lat(err_all, err_s, err_r)
    back_copies = {}
    for g in range(groups):
        arrive(err_copies, g)
        back = jnp.dot(rows_of(err_all, g), wdec_t[...], preferred_element_type=F32)
        back_buf[l, group[g]] = back.astype(BF16)
        back_copies[g] = to_lay(back_buf, g, back_s, back_r)
    errs = err_all[...].reshape(rows, wide)
    dec_out[...] = jnp.dot(code_t, errs, preferred_element_type=F32).astype(BF16)
    for g in range(groups):
        for copy in back_copies[g]:
            copy.wait_recv()
        lat_out[group[g]] = (total(back_buf, g) * slope[group[g]]).astype(BF16)
    for copy in started:
        copy.wait_send()


def finish(chunks, lat, acts_t, dec, lat_hbm, enc_hbm, dec_hbm, enc, sems):
    rows, lat_dev = lat.shape[0] * lat.shape[1], lat.shape[2]
    copies = [
        pltpu.make_async_copy(dec, dec_hbm, sems.at[0]),
        pltpu.make_async_copy(lat, lat_hbm, sems.at[1]),
    ]
    for copy in copies:
        copy.start()
    grad = lat[...].reshape(rows, lat_dev)
    tall = enc.shape[0] // chunks
    for c in range(chunks):
        cut = pl.ds(c * tall, tall)
        enc[cut] = jnp.dot(acts_t[cut], grad, preferred_element_type=F32).astype(BF16)
        copy = pltpu.make_async_copy(enc.at[cut], enc_hbm.at[cut], sems.at[2 + c])
        copy.start()
        copies.append(copy)
    for copy in copies:
        copy.wait()


def solution(mesh):
    n_lat, n_lay = mesh.shape["lat"], mesh.shape["lay"]

    def on_device(acts, w_enc, w_dec, b_enc, b_dec):
        row_dev, lay_dev, width = acts.shape
        lat_dev = w_enc.shape[2]
        wide, rows = lay_dev * width, n_lat * row_dev
        hbm = pl.BlockSpec(memory_space=pltpu.HBM)
        vmem = pl.BlockSpec(memory_space=pltpu.VMEM)
        dma = pltpu.SemaphoreType.DMA
        groups = 4 if n_lat & (n_lat - 1) == 0 and n_lat % 4 == 0 else 1
        part = rows // groups
        chunks = 5 if wide % 80 == 0 else 1
        lat_part, acts_t, dec_part = pl.pallas_call(
            functools.partial(step, n_lat, n_lay, groups),
            out_shape=[
                pltpu.VMEM((groups, part, lat_dev), BF16),
                pltpu.VMEM((wide, rows), BF16),
                pltpu.VMEM((lat_dev, wide), BF16),
            ],
            in_specs=[hbm, hbm, hbm, vmem, vmem],
            out_specs=[vmem, vmem, vmem],
            scratch_shapes=[
                pltpu.VMEM((n_lat, row_dev, wide), BF16),
                pltpu.VMEM((wide, lat_dev), BF16),
                pltpu.VMEM((lat_dev, wide), BF16),
                pltpu.VMEM((wide, lat_dev), BF16),
                pltpu.VMEM((n_lay, groups, part, lat_dev), BF16),
                pltpu.VMEM((n_lay, groups, part, lat_dev), BF16),
                pltpu.VMEM((n_lat, row_dev, wide), BF16),
                pltpu.VMEM((n_lat, row_dev, wide), BF16),
                pltpu.VMEM((n_lat, row_dev, wide), BF16),
                pltpu.VMEM((groups, part, lat_dev), BF16),
                pltpu.VMEM((groups, part, lat_dev), F32),
                dma((3,)),
                dma((n_lat,)), dma((n_lat,)),
                dma((groups, n_lay)), dma((groups, n_lay)),
                dma((n_lat,)), dma((n_lat,)),
                dma((n_lat,)), dma((n_lat,)),
                dma((groups, n_lay)), dma((groups, n_lay)),
            ],
            compiler_params=pltpu.CompilerParams(collective_id=0, has_side_effects=True),
            cost_estimate=pl.CostEstimate(
                flops=8 * rows * wide * lat_dev,
                bytes_accessed=4 * wide * lat_dev,
                transcendentals=0,
            ),
        )(
            acts.reshape(row_dev, wide),
            w_enc.reshape(wide, lat_dev),
            w_dec.reshape(lat_dev, wide),
            b_enc,
            b_dec.reshape(1, wide),
        )
        lat_grad, enc_grad, dec_grad = pl.pallas_call(
            functools.partial(finish, chunks),
            out_shape=[
                jax.ShapeDtypeStruct((groups, part, lat_dev), BF16),
                jax.ShapeDtypeStruct((wide, lat_dev), BF16),
                jax.ShapeDtypeStruct((lat_dev, wide), BF16),
            ],
            in_specs=[vmem, vmem, vmem],
            out_specs=[hbm, hbm, hbm],
            scratch_shapes=[pltpu.VMEM((wide, lat_dev), BF16), dma((2 + chunks,))],
            compiler_params=pltpu.CompilerParams(vmem_limit_bytes=8 * wide * lat_dev),
            cost_estimate=pl.CostEstimate(
                flops=2 * rows * wide * lat_dev,
                bytes_accessed=4 * wide * lat_dev,
                transcendentals=0,
            ),
        )(lat_part, acts_t, dec_part)
        return (
            lat_grad.reshape(rows, lat_dev),
            enc_grad.reshape(lay_dev, width, lat_dev),
            dec_grad.reshape(lat_dev, lay_dev, width),
        )

    in_specs = (
        P(("grp", "lat"), "lay", None),
        P("lay", None, "lat"),
        P("lat", "lay", None),
        P("lat"),
        P("lay", None),
    )
    out_specs = (P("grp", "lat"), P(("grp", "lay"), None, "lat"), P("lat", ("grp", "lay"), None))
    return jax.shard_map(
        on_device, mesh=mesh, in_specs=in_specs, out_specs=out_specs, check_vma=False
    )
```

time: 35.9 us -> 30.5 us (0.85)
  local copies, waits for them, and re-layouts: 4.7 us -> 0 us
  Pallas kernels: 30.3 us -> 29.7 us
    unnamed x5 -> x0, local copies, waits for them, and re-layouts: 4.7 us -> none
    pallas_call x1 -> x2, Pallas kernels: 30.3 us -> 29.7 us  [the longest x1 28.3 us: on_device(): pl.pallas_call(functools.partial(step, n_lat, n_lay, groups), out_shape=[...]
where the time goes in v2:
time: 30.5 us; the launch traced here: 30.3 us
  Pallas kernels  29.7 us (97%)
  between operations  0.64 us (2%)
    pallas_call x1, Pallas kernels, on_device(): pl.pallas_call(functools.partial(step, n_lat, n_lay, groups), out_shape=[...  28.3 us
    pallas_call x1, Pallas kernels, on_device(): pl.pallas_call(functools.partial(finish, chunks), out_shape=[jax.ShapeDty...  1.34 us

profile of v2, /device:TPU:0, one launch (start us, length us, event | category | flops | bytes accessed | tf_op | source)
XLA Modules:
  0.0 30.3 jit_solution(3504191365799288175)
XLA Ops:
  0.6 28.3 %shard_map.76 = (bf16[4,16,384]{2,1,0:T(8,128)(2,1)S(1)}, bf16[1280,64]{1,0:T(8,128)(2,1)S(1)}, bf16[384,1280]{1,0:T(8,128)(2,1)S(1)}) custom-call(bf16[16,1280]{1,0:T(8,128)(2,1)} %bitcast.8, bf16[1280,384]{1,0:T(8,128)(2,1)} %bitcast.6, bf16[384,1280]{1,0:T(8,128)(2,1)} %bitcast.7, f32[384]{0:T(512)} %benc_ref.1, f32[1,1280]{1,0:T(1,128)} %bdec_ref.1), custom_call_target="tpu_custom_call" | custom-call | flops 251658240 | bytes 1966080 | tf_op jit(solution)/shard_map/pallas_call | solution.py:193
  29.0 1.3 %shard_map.77 = (bf16[4,16,384]{2,1,0:T(8,128)(2,1)}, bf16[1280,384]{1,0:T(8,128)(2,1)}, bf16[384,1280]{1,0:T(8,128)(2,1)}) custom-call(bf16[4,16,384]{2,1,0:T(8,128)(2,1)S(1)} %get-tuple-element.9.lat, bf16[1280,64]{1,0:T(8,128)(2,1)S(1)} %get-tuple-element.10.acts_t, bf16[384,1280]{1,0:T(8,128)(2,1)S(1)} %get-tuple-element.11.dec), custom_call_target="tpu_custom_call" | custom-call | flops 62914560 | bytes 1966080 | tf_op jit(solution)/shard_map/pallas_call | solution.py:234

commit v3 on v2

--- a/solution.py
+++ b/solution.py
@@ -72,7 +72,7 @@
     def to_lat(buf, sent, received):
         return {
             j: send(buf.at[z], buf.at[z], sent.at[j], received.at[j], {"lat": dest(j)})
-            for j in reversed(range(1, n_lat))
+            for j in range(1, n_lat)
         }
 
     def to_lay(buf, g, sent, received):
@@ -125,14 +125,12 @@
         slope[group[g]] = jnp.where(x >= 0.0, 1.0, e) / (1.0 + e)
 
     for g in range(groups):
-        if g == groups - 1 and g:
-            decode(0)
         encode(g)
         if g == 0:
             load_dec.wait()
-            wdec_t[...] = wdec[...].astype(F32).T.astype(BF16)
-    for g in range(1 if groups > 1 else 0, groups):
+    for g in [*range(1, groups), 0]:
         decode(g)
+    wdec_t[...] = wdec[...].astype(F32).T.astype(BF16)
     acts_t[...] = acts_all[...].reshape(rows, wide).astype(F32).T.astype(BF16)
     code_t = code_all[...].reshape(rows, lat_dev).astype(F32).T.astype(BF16)
     err = bdec_ref[...] - acts_all[z].astype(F32) + rec_mine[z].astype(F32)

time: 30.5 us -> 29.3 us (0.961)
  Pallas kernels: 29.7 us -> 28.5 us
    pallas_call x1, Pallas kernels: 28.3 us -> 27.2 us  [on_device(): pl.pallas_call(functools.partial(step, n_lat, n_lay, groups), out_shape=[...]
where the time goes in v3:
time: 29.3 us; the launch traced here: 29.1 us
  Pallas kernels  28.5 us (97%)
  between operations  0.64 us (2%)
    pallas_call x1, Pallas kernels, on_device(): pl.pallas_call(functools.partial(step, n_lat, n_lay, groups), out_shape=[...  27.2 us
    pallas_call x1, Pallas kernels, on_device(): pl.pallas_call(functools.partial(finish, chunks), out_shape=[jax.ShapeDty...  1.34 us

profile of v3, /device:TPU:0, one launch (start us, length us, event | category | flops | bytes accessed | tf_op | source)
XLA Modules:
  0.0 29.1 jit_solution(7670284543554389979)
XLA Ops:
  0.6 27.2 %shard_map.76 = (bf16[4,16,384]{2,1,0:T(8,128)(2,1)S(1)}, bf16[1280,64]{1,0:T(8,128)(2,1)S(1)}, bf16[384,1280]{1,0:T(8,128)(2,1)S(1)}) custom-call(bf16[16,1280]{1,0:T(8,128)(2,1)} %bitcast.8, bf16[1280,384]{1,0:T(8,128)(2,1)} %bitcast.6, bf16[384,1280]{1,0:T(8,128)(2,1)} %bitcast.7, f32[384]{0:T(512)} %benc_ref.1, f32[1,1280]{1,0:T(1,128)} %bdec_ref.1), custom_call_target="tpu_custom_call" | custom-call | flops 251658240 | bytes 1966080 | tf_op jit(solution)/shard_map/pallas_call | solution.py:191
  27.8 1.3 %shard_map.77 = (bf16[4,16,384]{2,1,0:T(8,128)(2,1)}, bf16[1280,384]{1,0:T(8,128)(2,1)}, bf16[384,1280]{1,0:T(8,128)(2,1)}) custom-call(bf16[4,16,384]{2,1,0:T(8,128)(2,1)S(1)} %get-tuple-element.9.lat, bf16[1280,64]{1,0:T(8,128)(2,1)S(1)} %get-tuple-element.10.acts_t, bf16[384,1280]{1,0:T(8,128)(2,1)S(1)} %get-tuple-element.11.dec), custom_call_target="tpu_custom_call" | custom-call | flops 62914560 | bytes 1966080 | tf_op jit(solution)/shard_map/pallas_call | solution.py:232
